TPU v7x, 32 devices: a whole 2x2x4 slice. The times are simulated.
32 devices in a mesh: group: 4 (over y, core), member: 8 (over z, x).
Axes of the slice: x: 2, y: 2, z: 4, core: 2. Of those that a mesh axis runs over, the one named last changes fastest.
Arguments:
- off_tiles: bfloat16 [64, 8, 128, 128], P(('group', 'member')), may hold values from -0.1875 to 0.1875
- off_cols: int32 [64, 8], P(('group', 'member')), may hold values from 0 to 17
- member_send: int32 [32, 8, 1], P(('group', 'member')), may hold values from 0 to 1
- group_send: int32 [32, 4], P(('group', 'member')), may hold values from 0 to 1
- diag_tiles: bfloat16 [64, 128, 128], P(('group', 'member')), may hold values from -1 to 9
- smoother: bfloat16 [64, 128, 128], P(('group', 'member')), may hold values from -1 to 1
- agg_map: int32 [64], P(('group', 'member')), may hold values from 0 to 1
- prolong: bfloat16 [64, 128, 128], P(('group', 'member')), may hold values from -0.5 to 0.5
- coarse_inv: bfloat16 [1024, 1024], P(None, 'group'), may hold values from -0.03125 to 0.03125
- krylov_basis: bfloat16 [64, 32, 128], P(('group', 'member')), may hold values from -24 to 24, as said below
Outputs:
- preconditioned: bfloat16 [64, 8, 128], P(('group', 'member'))
- coefficients: float32 [32, 8], replicated
- gram_matrix: float32 [8, 8], replicated
- new_block: float32 [64, 8, 128], P(('group', 'member'))
Inputs may be any that keep to these rules, and one draw needn't show every extreme that they name: `off_cols`: entries below 2 name the device's own row tiles; entry 2 + p + s names slot s of what member p of the same group sends; the last 8 entries name what the groups below and above send. `member_send`: entry [d, p, s] is the local row tile that device d sends to member p of its group in slot s. `group_send`: entry [d, s] is the local row tile that device d sends, in slot s, to the same member of the groups below and above. `krylov_basis`: the 32 basis vectors are orthonormal, up to bfloat16 rounding, under the inner product (1 / 8192) times the sum over all rows.
All inputs are finite; a program needn't handle non-finite values.
Results may differ from a plain program's by a relative error of at most 0.02.
Values may be sent and summed in bfloat16 or wider, within the bound.
No kernel may reach another device: no remote copies, remote signals or barrier semaphores. Data moves between devices by JAX's collectives and lax.ppermute only.
A program may use at most 64 MiB of HBM per device.

v0:
```python
import jax
import jax.numpy as jnp
from jax import lax
from jax.sharding import PartitionSpec as P

TILE = 128
NVEC = 8
GH = 1
CTG = 2


def extended_2(cells, sides, width):
    for axis, dim in sides:
        count = lax.axis_size(axis)
        ends = count - 1
        head = lax.slice_in_dim(cells, 0, width, axis=dim)
        tail = lax.slice_in_dim(cells, cells.shape[dim] - width, cells.shape[dim], axis=dim)
        cells = jnp.concatenate(
            [
                lax.ppermute(tail, axis, [(i, (i + 1) % count) for i in range(ends)]),
                cells,
                lax.ppermute(head, axis, [((i + 1) % count, i) for i in range(ends)]),
            ],
            axis=dim,
        )
    return cells


def extend_tiles(values, member_send, group_send, members):
    outgoing = values[member_send[0].reshape(-1)].reshape(members, GH, NVEC, TILE)
    arrived = lax.all_to_all(outgoing, "member", split_axis=0, concat_axis=0, tiled=True).reshape(
        members * GH, NVEC, TILE
    )
    rim_tiles = values[group_send[0]][None]
    beside = extended_2(rim_tiles, (("group", 0),), 1)
    return jnp.concatenate([values, arrived, beside[0], beside[2]], axis=0)


def operate(values, off_tiles, off_cols, diag_tiles, member_send, group_send, members):
    extended = extend_tiles(values, member_send, group_send, members)
    picked = extended[off_cols]
    far_part = jnp.einsum("tkcj,tkji->tci", picked, off_tiles, preferred_element_type=jnp.float32)
    near_part = jnp.einsum("tcj,tji->tci", values, diag_tiles, preferred_element_type=jnp.float32)
    return near_part + far_part


def tilewise(left_side, tiles):
    return jnp.einsum("tcj,tji->tci", left_side, tiles, preferred_element_type=jnp.float32)


def exact_product(form, first_operand, second_operand):
    return jnp.einsum(form, first_operand, second_operand, precision=lax.Precision.HIGHEST)


def local(
    off_tiles,
    off_cols,
    member_send,
    group_send,
    diag_tiles,
    smoother,
    agg_map,
    prolong,
    coarse_inv,
    krylov_basis,
):
    members = lax.axis_size("member")
    groups = lax.axis_size("group")
    tiles_dev = diag_tiles.shape[0]
    rows_all = tiles_dev * TILE * members * groups
    scale_rows = 1.0 / rows_all

    def apply_operator(values):
        return operate(values, off_tiles, off_cols, diag_tiles, member_send, group_send, members)

    last_block = krylov_basis[:, krylov_basis.shape[1] - NVEC :, :]
    block_wide = last_block.astype(jnp.float32)
    first = tilewise(last_block, smoother).astype(jnp.bfloat16)
    residual_one = (block_wide - apply_operator(first)).astype(jnp.bfloat16)
    pieces = jnp.einsum("tci,tji->tcj", residual_one, prolong, preferred_element_type=jnp.float32)
    selector = (agg_map[:, None] == jnp.arange(CTG, dtype=jnp.int32)[None, :]).astype(jnp.float32)
    coarse_part = exact_product("ta,tcj->acj", selector, pieces)
    spread = jnp.zeros((groups, CTG, NVEC, TILE), jnp.float32)
    spread = lax.dynamic_update_slice(spread, coarse_part[None], (lax.axis_index("group"), 0, 0, 0))
    coarse_all = lax.psum(spread, ("group", "member")).reshape(groups * CTG, NVEC, TILE)
    coarse_round = coarse_all.astype(jnp.bfloat16)
    columns = coarse_inv.reshape(groups * CTG, TILE, CTG * TILE)
    correction = jnp.einsum(
        "acj,ajo->co", coarse_round, columns, preferred_element_type=jnp.float32
    )
    correction = correction.astype(jnp.bfloat16).reshape(NVEC, CTG, TILE)
    chosen = jnp.einsum(
        "ta,cak->tck", selector.astype(jnp.bfloat16), correction, preferred_element_type=jnp.float32
    )
    second = (first.astype(jnp.float32) + tilewise(chosen.astype(jnp.bfloat16), prolong)).astype(
        jnp.bfloat16
    )
    residual_two = (block_wide - apply_operator(second)).astype(jnp.bfloat16)
    preconditioned = (second.astype(jnp.float32) + tilewise(residual_two, smoother)).astype(
        jnp.bfloat16
    )
    applied = apply_operator(preconditioned).astype(jnp.bfloat16)
    coeff_part = (
        jnp.einsum("tpi,tci->pc", krylov_basis, applied, preferred_element_type=jnp.float32)
        * scale_rows
    )
    basis_wide = krylov_basis.astype(jnp.float32)
    self_part = (
        jnp.einsum("tci,tdi->cd", applied, applied, preferred_element_type=jnp.float32) * scale_rows
    )
    basis_part = (
        jnp.einsum("tpi,tqi->pq", krylov_basis, krylov_basis, preferred_element_type=jnp.float32)
        * scale_rows
    )
    coefficients, self_total, basis_total = lax.psum(
        (coeff_part, self_part, basis_part), ("group", "member")
    )
    remainder = applied.astype(jnp.float32) - exact_product("pc,tpi->tci", coefficients, basis_wide)
    cross = exact_product("pc,pd->cd", coefficients, coefficients)
    weighted = exact_product("pq,qd->pd", basis_total, coefficients)
    gram_matrix = self_total - 2.0 * cross + exact_product("pc,pd->cd", coefficients, weighted)
    factor = jnp.linalg.cholesky(gram_matrix)
    inverse = lax.linalg.triangular_solve(
        factor, jnp.eye(NVEC, dtype=jnp.float32), left_side=True, lower=True
    )
    new_block = exact_product("cd,tdi->tci", inverse, remainder)
    return (preconditioned, coefficients, gram_matrix, new_block)


def solution(mesh):
    placed = (
        P(("group", "member"), None, None, None),
        P(("group", "member"), None),
        P(("group", "member"), None, None),
        P(("group", "member"), None),
        P(("group", "member"), None, None),
        P(("group", "member"), None, None),
        P(("group", "member")),
        P(("group", "member"), None, None),
        P(None, "group"),
        P(("group", "member"), None, None),
    )
    return jax.shard_map(
        local,
        mesh=mesh,
        in_specs=placed,
        out_specs=(
            P(("group", "member"), None, None),
            P(),
            P(),
            P(("group", "member"), None, None),
        ),
        check_vma=False,
    )
```

profile of v0, /device:TPU:0, one launch (start us, length us, event | category | flops | bytes accessed | tf_op | source)
XLA Modules:
  0.0 144.9 jit_solution(4221777477460338780)
XLA Ops:
  0.6 0.7 fusion.33
  1.4 1.0 convolution_convert_fusion
  2.9 2.4 %collective-permute-start = (bf16[1,4,8,128]{3,2,1,0:T(8,128)(2,1)S(1)}, bf16[1,4,8,128]{3,2,1,0:T(8,128)(2,1)S(1)}, u32[]{:S(2)}, u32[]{:S(2)}) collective-permute-start(bf16[1,4,8,128]{3,2,1,0:T(8,128)(2,1)S(1)} %bitcast.145), channel_id=1, source_target_pairs={{0,8},{8,16},{16,24},{1,9},{9,17},{17,25},{2,10},{10,18},{18,26},{... | collective-permute-start | bytes 24584 | tf_op jit(solution)/shard_map/ppermute | solution.py:20
  5.3 1.3 collective-permute-start.1
  6.7 1.2 gather_fusion
  7.8 6.8 %all-to-all-start = ((bf16[8,1,8,128]{3,2,1,0:T(8,128)(2,1)}), bf16[8,1,8,128]{3,2,1,0:T(8,128)(2,1)S(1)}, u32[]{:S(2)}, u32[]{:S(2)}) async-start(bf16[8,1,8,128]{3,2,1,0:T(8,128)(2,1)} %bitcast.5), calls=%async_computation | async-start | bytes 32768 | tf_op jit(solution)/shard_map/all_to_all | solution.py:31
  14.7 6.5 %all-to-all-done = bf16[8,1,8,128]{3,2,1,0:T(8,128)(2,1)S(1)} async-done(((bf16[8,1,8,128]{3,2,1,0:T(8,128)(2,1)}), bf16[8,1,8,128]{3,2,1,0:T(8,128)(2,1)S(1)}, u32[]{:S(2)}, u32[]{:S(2)}) %all-to-all-start) | async-done | bytes 16416 | tf_op jit(solution)/shard_map/all_to_all | solution.py:31
  21.8 1.3 convolution_bitcast_fusion.7
  23.9 41.0 %psum.28 = bf16[4,2,8,128]{3,1,2,0:T(2,128)(2,1)S(1)} all-reduce(f32[4,2,8,128]{3,1,2,0:T(2,128)S(1)} %fusion.3), channel_id=1, replica_groups=mesh['group'=4,'member'=8] {'group','member'}, use_global_device_ids=true, to_apply=%region_0.0 | all-reduce | flops 8192 | bytes 49152 | tf_op jit(solution)/shard_map/psum | solution.py:85
  65.4 1.2 gather_fusion.3
  66.6 4.5 %all-to-all-start.1 = ((bf16[8,1,8,128]{3,2,1,0:T(8,128)(2,1)}), bf16[8,1,8,128]{3,2,1,0:T(8,128)(2,1)S(1)}, u32[]{:S(2)}, u32[]{:S(2)}) async-start(bf16[8,1,8,128]{3,2,1,0:T(8,128)(2,1)} %bitcast.21), calls=%async_computation.1 | async-start | bytes 32768 | tf_op jit(solution)/shard_map/all_to_all | solution.py:31
  71.6 1.3 collective-permute-start.2
  72.9 1.3 collective-permute-start.3
  74.3 3.6 %collective-permute-done.3 = bf16[1,4,8,128]{3,2,1,0:T(8,128)(2,1)S(1)} collective-permute-done((bf16[1,4,8,128]{3,2,1,0:T(8,128)(2,1)S(1)}, bf16[1,4,8,128]{3,2,1,0:T(8,128)(2,1)S(1)}, u32[]{:S(2)}, u32[]{:S(2)}) %collective-permute-start.3) | collective-permute-done | bytes 8224 | tf_op jit(solution)/shard_map/ppermute | solution.py:22
  78.6 0.6 copy-done.5
  79.5 1.2 gather_fusion.6
  81.2 4.3 %collective-permute-start.4 = (bf16[1,4,8,128]{3,2,1,0:T(8,128)(2,1)S(1)}, bf16[1,4,8,128]{3,2,1,0:T(8,128)(2,1)S(1)}, u32[]{:S(2)}, u32[]{:S(2)}) collective-permute-start(bf16[1,4,8,128]{3,2,1,0:T(8,128)(2,1)S(1)} %bitcast.147), channel_id=1, source_target_pairs={{0,8},{8,16},{16,24},{1,9},{9,17},{17,25},{2,10},{10,18},{18,26},{... | collective-permute-start | bytes 24584 | tf_op jit(solution)/shard_map/ppermute | solution.py:20
  85.5 1.3 collective-permute-start.5
  86.8 6.0 %all-to-all-start.2 = ((bf16[8,1,8,128]{3,2,1,0:T(8,128)(2,1)}), bf16[8,1,8,128]{3,2,1,0:T(8,128)(2,1)S(1)}, u32[]{:S(2)}, u32[]{:S(2)}) async-start(bf16[8,1,8,128]{3,2,1,0:T(8,128)(2,1)} %bitcast.30), calls=%async_computation.2 | async-start | bytes 32768 | tf_op jit(solution)/shard_map/all_to_all | solution.py:31
  93.0 6.5 %all-to-all-done.2 = bf16[8,1,8,128]{3,2,1,0:T(8,128)(2,1)S(1)} async-done(((bf16[8,1,8,128]{3,2,1,0:T(8,128)(2,1)}), bf16[8,1,8,128]{3,2,1,0:T(8,128)(2,1)S(1)}, u32[]{:S(2)}, u32[]{:S(2)}) %all-to-all-start.2) | async-done | bytes 16416 | tf_op jit(solution)/shard_map/all_to_all | solution.py:31
  100.6 39.3 %all-reduce = (f32[32,8]{0,1:T(8,128)S(1)}, f32[8,8]{0,1:T(8,128)S(1)}, f32[32,32]{1,0:T(8,128)S(1)}) all-reduce(f32[32,8]{0,1:T(8,128)S(1)} %fusion.15, f32[8,8]{0,1:T(8,128)S(1)} %fusion.13, f32[32,32]{1,0:T(8,128)S(1)} %fusion), channel_id=1, replica_groups=mesh['group'=4,'member'=8] {'group','member'}, use_global_device_ids=true, to_apply=%region_1.0 | all-reduce | flops 1344 | bytes 10752 | tf_op jit(solution)/shard_map/psum | solution.py:115
  141.3 0.7 cholesky.17
  142.7 0.6 fusion.20
  144.2 0.8 convolution_bitcast_fusion.1
  (68 shorter events, 9.0 us)
Async XLA Ops:
  0.6 64.3 %copy-start = (bf16[1024,256]{1,0:T(8,128)(2,1)S(1)}, bf16[1024,256]{1,0:T(8,128)(2,1)}, u32[]{:S(2)}) copy-start(bf16[1024,256]{1,0:T(8,128)(2,1)} %param.18) | copy-start | bytes 1572868
  2.9 3.7 %copy-start.10 = (s32[1,8,1]{1,2,0:T(1,128)S(1)}, s32[1,8,1]{1,2,0:T(1,128)}, u32[]{:S(2)}) copy-start(s32[1,8,1]{1,2,0:T(1,128)} %param.12) | copy-start | bytes 100
  2.9 11.8 %collective-permute-start = (bf16[1,4,8,128]{3,2,1,0:T(8,128)(2,1)S(1)}, bf16[1,4,8,128]{3,2,1,0:T(8,128)(2,1)S(1)}, u32[]{:S(2)}, u32[]{:S(2)}) collective-permute-start(bf16[1,4,8,128]{3,2,1,0:T(8,128)(2,1)S(1)} %bitcast.145), channel_id=1, source_target_pairs={{0,8},{8,16},{16,24},{1,9},{9,17},{17,25},{2,10},{10,18},{18,26},{... | collective-permute-start | bytes 24584 | tf_op jit(solution)/shard_map/ppermute | solution.py:20
  5.3 9.4 %collective-permute-start.1 = (bf16[1,4,8,128]{3,2,1,0:T(8,128)(2,1)S(1)}, bf16[1,4,8,128]{3,2,1,0:T(8,128)(2,1)S(1)}, u32[]{:S(2)}, u32[]{:S(2)}) collective-permute-start(bf16[1,4,8,128]{3,2,1,0:T(8,128)(2,1)S(1)} %bitcast.146), channel_id=1, source_target_pairs={{8,0},{16,8},{24,16},{9,1},{17,9},{25,17},{10,2},{18,10},{26,18},{... | collective-permute-start | bytes 24584 | tf_op jit(solution)/shard_map/ppermute | solution.py:22
  7.8 6.8 %copy-start.9 = (s32[2,8]{1,0:T(2,128)S(1)}, s32[2,8]{1,0:T(2,128)}, u32[]{:S(2)}) copy-start(s32[2,8]{1,0:T(2,128)} %param.11) | copy-start | bytes 196
  7.8 13.3 %all-to-all-start = ((bf16[8,1,8,128]{3,2,1,0:T(8,128)(2,1)}), bf16[8,1,8,128]{3,2,1,0:T(8,128)(2,1)S(1)}, u32[]{:S(2)}, u32[]{:S(2)}) async-start(bf16[8,1,8,128]{3,2,1,0:T(8,128)(2,1)} %bitcast.5), calls=%async_computation | async-start | bytes 32768 | tf_op jit(solution)/shard_map/all_to_all | solution.py:31
  21.8 1.3 copy-start.2
  21.8 1.3 copy-start.3
  21.8 1.3 copy-start.6
  23.1 0.7 copy-start.11
  23.3 55.1 %copy-start.1 = (bf16[2,8,128,128]{3,2,1,0:T(8,128)(2,1)S(1)}, bf16[2,8,128,128]{3,2,1,0:T(8,128)(2,1)}, u32[]{:S(2)}) copy-start(bf16[2,8,128,128]{3,2,1,0:T(8,128)(2,1)} %param.10) | copy-start | bytes 1572868
  66.6 11.2 %all-to-all-start.1 = ((bf16[8,1,8,128]{3,2,1,0:T(8,128)(2,1)}), bf16[8,1,8,128]{3,2,1,0:T(8,128)(2,1)S(1)}, u32[]{:S(2)}, u32[]{:S(2)}) async-start(bf16[8,1,8,128]{3,2,1,0:T(8,128)(2,1)} %bitcast.21), calls=%async_computation.1 | async-start | bytes 32768 | tf_op jit(solution)/shard_map/all_to_all | solution.py:31
  71.6 2.6 %collective-permute-start.2 = (bf16[1,4,8,128]{3,2,1,0:T(8,128)(2,1)S(1)}, bf16[1,4,8,128]{3,2,1,0:T(8,128)(2,1)S(1)}, u32[]{:S(2)}, u32[]{:S(2)}) collective-permute-start(bf16[1,4,8,128]{3,2,1,0:T(8,128)(2,1)S(1)} %bitcast.149), channel_id=1, source_target_pairs={{0,8},{8,16},{16,24},{1,9},{9,17},{17,25},{2,10},{10,18},{18,26},{... | collective-permute-start | bytes 24584 | tf_op jit(solution)/shard_map/ppermute | solution.py:20
  72.9 4.9 %collective-permute-start.3 = (bf16[1,4,8,128]{3,2,1,0:T(8,128)(2,1)S(1)}, bf16[1,4,8,128]{3,2,1,0:T(8,128)(2,1)S(1)}, u32[]{:S(2)}, u32[]{:S(2)}) collective-permute-start(bf16[1,4,8,128]{3,2,1,0:T(8,128)(2,1)S(1)} %bitcast.150), channel_id=1, source_target_pairs={{8,0},{16,8},{24,16},{9,1},{17,9},{25,17},{10,2},{18,10},{26,18},{... | collective-permute-start | bytes 24584 | tf_op jit(solution)/shard_map/ppermute | solution.py:22
  78.4 0.8 copy-start.5
  79.5 20.7 %copy-start.4 = (bf16[2,8,128]{2,1,0:T(8,128)(2,1)}, bf16[2,8,128]{2,1,0:T(8,128)(2,1)S(1)}, u32[]{:S(2)}) copy-start(bf16[2,8,128]{2,1,0:T(8,128)(2,1)S(1)} %fusion.9) | copy-start | bytes 12292
  81.2 11.7 %collective-permute-start.4 = (bf16[1,4,8,128]{3,2,1,0:T(8,128)(2,1)S(1)}, bf16[1,4,8,128]{3,2,1,0:T(8,128)(2,1)S(1)}, u32[]{:S(2)}, u32[]{:S(2)}) collective-permute-start(bf16[1,4,8,128]{3,2,1,0:T(8,128)(2,1)S(1)} %bitcast.147), channel_id=1, source_target_pairs={{0,8},{8,16},{16,24},{1,9},{9,17},{17,25},{2,10},{10,18},{18,26},{... | collective-permute-start | bytes 24584 | tf_op jit(solution)/shard_map/ppermute | solution.py:20
  85.5 7.4 %collective-permute-start.5 = (bf16[1,4,8,128]{3,2,1,0:T(8,128)(2,1)S(1)}, bf16[1,4,8,128]{3,2,1,0:T(8,128)(2,1)S(1)}, u32[]{:S(2)}, u32[]{:S(2)}) collective-permute-start(bf16[1,4,8,128]{3,2,1,0:T(8,128)(2,1)S(1)} %bitcast.148), channel_id=1, source_target_pairs={{8,0},{16,8},{24,16},{9,1},{17,9},{25,17},{10,2},{18,10},{26,18},{... | collective-permute-start | bytes 24584 | tf_op jit(solution)/shard_map/ppermute | solution.py:22
  86.8 12.6 %all-to-all-start.2 = ((bf16[8,1,8,128]{3,2,1,0:T(8,128)(2,1)}), bf16[8,1,8,128]{3,2,1,0:T(8,128)(2,1)S(1)}, u32[]{:S(2)}, u32[]{:S(2)}) async-start(bf16[8,1,8,128]{3,2,1,0:T(8,128)(2,1)} %bitcast.30), calls=%async_computation.2 | async-start | bytes 32768 | tf_op jit(solution)/shard_map/all_to_all | solution.py:31
  139.8 0.6 copy-start.7
  140.7 0.6 copy-start.8
where the time goes:
time: 146 us; the launch traced here: 145 us
  blocking collectives  80.3 us (55%)
  starting transfers between devices  29.1 us (20%)
  waiting for transfers between devices  16.5 us (11%)
  local copies, waits for them, and re-layouts  8.97 us (6%)
  matrix products  5.74 us (4%)
  other arithmetic  3.44 us (2%)
    psum x1, blocking collectives, local(): lax.psum(spread, ('group', 'member')).reshape(groups * CTG, NVEC, TILE)  41 us
    psum x1, blocking collectives, local(): lax.psum((coeff_part, self_part, basis_part), ('group', 'member'))  39.3 us
    all_to_all x3, starting transfers between devices, extend_tiles(): lax.all_to_all(outgoing, 'member', split_axis=0, concat_axis=0, tiled=True)  17.3 us
    all_to_all x3, waiting for transfers between devices, extend_tiles(): lax.all_to_all(outgoing, 'member', split_axis=0, concat_axis=0, tiled=True)  12.9 us
    ppermute x3, starting transfers between devices, extended_2(): lax.ppermute(tail, axis, [(i, (i + 1) % count) for i in range(ends)])  7.99 us
    ppermute x3, starting transfers between devices, extended_2(): lax.ppermute(head, axis, [((i + 1) % count, i) for i in range(ends)])  3.88 us
    ppermute x3, waiting for transfers between devices, extended_2(): lax.ppermute(head, axis, [((i + 1) % count, i) for i in range(ends)])  3.57 us
    gather x3, local copies, waits for them, and re-layouts, extend_tiles(): values[member_send[0].reshape(-1)].reshape(members, GH, NVEC, TILE)  3.5 us
  transfers between devices with their start and end apart: 9, of which 3 were waited for; matrix products, arithmetic and copies ran while one was open for 1% of the time, Pallas kernels for 0%

commit v1 on v0

--- a/solution.py
+++ b/solution.py
@@ -82,7 +82,9 @@
     coarse_part = exact_product("ta,tcj->acj", selector, pieces)
     spread = jnp.zeros((groups, CTG, NVEC, TILE), jnp.float32)
     spread = lax.dynamic_update_slice(spread, coarse_part[None], (lax.axis_index("group"), 0, 0, 0))
-    coarse_all = lax.psum(spread, ("group", "member")).reshape(groups * CTG, NVEC, TILE)
+    coarse_all = jnp.sum(lax.all_gather(spread, ("group", "member")), axis=0).reshape(
+        groups * CTG, NVEC, TILE
+    )
     coarse_round = coarse_all.astype(jnp.bfloat16)
     columns = coarse_inv.reshape(groups * CTG, TILE, CTG * TILE)
     correction = jnp.einsum(

time: 146 us -> 173 us (1.18)
  waiting for transfers between devices: 16.5 us -> 69.6 us
  blocking collectives: 80.3 us -> 39.3 us
  between operations: 0.89 us -> 14.3 us
    all_gather x0 -> x1, waiting for transfers between devices: none -> 53.8 us  [local(): lax.all_gather(spread, ('group', 'member'))]
    psum x1 -> x0, blocking collectives: 41 us -> none  [local(): lax.psum(spread, ('group', 'member')).reshape(groups * CTG, NVEC, TILE)]
  transfers between devices with their start and end apart: 9 -> 10, of which waited for: 3 -> 5; matrix products, arithmetic and copies ran while one was open for 1% -> 1% of each run, Pallas kernels for 0% -> 0%
where the time goes in v1:
time: 173 us; the launch traced here: 172 us
  waiting for transfers between devices  69.6 us (40%)
  blocking collectives  39.3 us (23%)
  starting transfers between devices  28.9 us (17%)
  between operations  14.3 us (8%)
  local copies, waits for them, and re-layouts  9.56 us (6%)
  matrix products  5.8 us (3%)
  other arithmetic  4.73 us (3%)
    all_gather x1, waiting for transfers between devices, local(): lax.all_gather(spread, ('group', 'member'))  53.8 us
    psum x1, blocking collectives, local(): lax.psum((coeff_part, self_part, basis_part), ('group', 'member'))  39.3 us
    all_to_all x3, starting transfers between devices, extend_tiles(): lax.all_to_all(outgoing, 'member', split_axis=0, concat_axis=0, tiled=True)  17.1 us
    all_to_all x3, waiting for transfers between devices, extend_tiles(): lax.all_to_all(outgoing, 'member', split_axis=0, concat_axis=0, tiled=True)  13.5 us
    ppermute x3, starting transfers between devices, extended_2(): lax.ppermute(tail, axis, [(i, (i + 1) % count) for i in range(ends)])  7.88 us
    ppermute x3, starting transfers between devices, extended_2(): lax.ppermute(head, axis, [((i + 1) % count, i) for i in range(ends)])  3.88 us
    gather x3, local copies, waits for them, and re-layouts, extend_tiles(): values[member_send[0].reshape(-1)].reshape(members, GH, NVEC, TILE)  3.49 us
  transfers between devices with their start and end apart: 10, of which 5 were waited for; matrix products, arithmetic and copies ran while one was open for 1% of the time, Pallas kernels for 0%

profile of v1, /device:TPU:0, one launch (start us, length us, event | category | flops | bytes accessed | tf_op | source)
XLA Modules:
  0.0 172.1 jit_solution(7872630435807660716)
XLA Ops:
  7.2 0.7 fusion.32
  7.9 1.0 convolution_convert_fusion.1
  9.5 2.4 %collective-permute-start = (bf16[1,4,8,128]{3,2,1,0:T(8,128)(2,1)S(1)}, bf16[1,4,8,128]{3,2,1,0:T(8,128)(2,1)S(1)}, u32[]{:S(2)}, u32[]{:S(2)}) collective-permute-start(bf16[1,4,8,128]{3,2,1,0:T(8,128)(2,1)S(1)} %bitcast.143), channel_id=1, source_target_pairs={{0,8},{8,16},{16,24},{1,9},{9,17},{17,25},{2,10},{10,18},{18,26},{... | collective-permute-start | bytes 24584 | tf_op jit(solution)/shard_map/ppermute | solution.py:20
  11.9 1.3 collective-permute-start.1
  13.2 1.2 gather_fusion
  14.4 6.8 %all-to-all-start = ((bf16[8,1,8,128]{3,2,1,0:T(8,128)(2,1)}), bf16[8,1,8,128]{3,2,1,0:T(8,128)(2,1)S(1)}, u32[]{:S(2)}, u32[]{:S(2)}) async-start(bf16[8,1,8,128]{3,2,1,0:T(8,128)(2,1)} %bitcast.5), calls=%async_computation | async-start | bytes 32768 | tf_op jit(solution)/shard_map/all_to_all | solution.py:31
  21.3 6.4 %all-to-all-done = bf16[8,1,8,128]{3,2,1,0:T(8,128)(2,1)S(1)} async-done(((bf16[8,1,8,128]{3,2,1,0:T(8,128)(2,1)}), bf16[8,1,8,128]{3,2,1,0:T(8,128)(2,1)S(1)}, u32[]{:S(2)}, u32[]{:S(2)}) %all-to-all-start) | async-done | bytes 16416 | tf_op jit(solution)/shard_map/all_to_all | solution.py:31
  28.3 1.3 convolution_bitcast_fusion.7
  31.2 53.8 %all-gather.2.cloned.1.call-done = f32[32,4,2,8,128]{4,3,2,1,0:T(8,128)} async-done(((f32[1,4,2,8,128]{4,3,2,1,0:T(8,128)}), f32[32,4,2,8,128]{4,3,2,1,0:T(8,128)}) %all-gather.2.cloned.1.call-update) | async-done | bytes 1048592 | tf_op jit(solution)/shard_map/all_gather | solution.py:85
  85.0 1.3 reduce_sum.9
  86.8 1.2 gather_fusion.3
  88.0 4.3 %all-to-all-start.1 = ((bf16[8,1,8,128]{3,2,1,0:T(8,128)(2,1)}), bf16[8,1,8,128]{3,2,1,0:T(8,128)(2,1)S(1)}, u32[]{:S(2)}, u32[]{:S(2)}) async-start(bf16[8,1,8,128]{3,2,1,0:T(8,128)(2,1)} %bitcast.21), calls=%async_computation.1 | async-start | bytes 32768 | tf_op jit(solution)/shard_map/all_to_all | solution.py:31
  92.9 1.8 %collective-permute-start.2 = (bf16[1,4,8,128]{3,2,1,0:T(8,128)(2,1)S(1)}, bf16[1,4,8,128]{3,2,1,0:T(8,128)(2,1)S(1)}, u32[]{:S(2)}, u32[]{:S(2)}) collective-permute-start(bf16[1,4,8,128]{3,2,1,0:T(8,128)(2,1)S(1)} %bitcast.147), channel_id=1, source_target_pairs={{0,8},{8,16},{16,24},{1,9},{9,17},{17,25},{2,10},{10,18},{18,26},{... | collective-permute-start | bytes 24584 | tf_op jit(solution)/shard_map/ppermute | solution.py:20
  94.7 1.3 collective-permute-start.3
  96.0 2.2 %collective-permute-done.3 = bf16[1,4,8,128]{3,2,1,0:T(8,128)(2,1)S(1)} collective-permute-done((bf16[1,4,8,128]{3,2,1,0:T(8,128)(2,1)S(1)}, bf16[1,4,8,128]{3,2,1,0:T(8,128)(2,1)S(1)}, u32[]{:S(2)}, u32[]{:S(2)}) %collective-permute-start.3) | collective-permute-done | bytes 8224 | tf_op jit(solution)/shard_map/ppermute | solution.py:22
  98.2 0.7 all-to-all-done.1
  100.6 1.2 gather_fusion.6
  102.3 3.6 %collective-permute-start.4 = (bf16[1,4,8,128]{3,2,1,0:T(8,128)(2,1)S(1)}, bf16[1,4,8,128]{3,2,1,0:T(8,128)(2,1)S(1)}, u32[]{:S(2)}, u32[]{:S(2)}) collective-permute-start(bf16[1,4,8,128]{3,2,1,0:T(8,128)(2,1)S(1)} %bitcast.145), channel_id=1, source_target_pairs={{0,8},{8,16},{16,24},{1,9},{9,17},{17,25},{2,10},{10,18},{18,26},{... | collective-permute-start | bytes 24584 | tf_op jit(solution)/shard_map/ppermute | solution.py:20
  105.9 1.3 collective-permute-start.5
  107.2 6.0 %all-to-all-start.2 = ((bf16[8,1,8,128]{3,2,1,0:T(8,128)(2,1)}), bf16[8,1,8,128]{3,2,1,0:T(8,128)(2,1)S(1)}, u32[]{:S(2)}, u32[]{:S(2)}) async-start(bf16[8,1,8,128]{3,2,1,0:T(8,128)(2,1)} %bitcast.30), calls=%async_computation.2 | async-start | bytes 32768 | tf_op jit(solution)/shard_map/all_to_all | solution.py:31
  113.4 6.5 %all-to-all-done.2 = bf16[8,1,8,128]{3,2,1,0:T(8,128)(2,1)S(1)} async-done(((bf16[8,1,8,128]{3,2,1,0:T(8,128)(2,1)}), bf16[8,1,8,128]{3,2,1,0:T(8,128)(2,1)S(1)}, u32[]{:S(2)}, u32[]{:S(2)}) %all-to-all-start.2) | async-done | bytes 16416 | tf_op jit(solution)/shard_map/all_to_all | solution.py:31
  121.0 39.3 %all-reduce = (f32[32,8]{0,1:T(8,128)S(1)}, f32[8,8]{0,1:T(8,128)S(1)}, f32[32,32]{1,0:T(8,128)S(1)}) all-reduce(f32[32,8]{0,1:T(8,128)S(1)} %fusion.14, f32[8,8]{0,1:T(8,128)S(1)} %fusion.12, f32[32,32]{1,0:T(8,128)S(1)} %fusion), channel_id=1, replica_groups=mesh['group'=4,'member'=8] {'group','member'}, use_global_device_ids=true, to_apply=%region_1.0 | all-reduce | flops 1344 | bytes 10752 | tf_op jit(solution)/shard_map/psum | solution.py:117
  161.6 0.7 cholesky.17
  164.5 0.8 convolution_bitcast_fusion.1
  (73 shorter events, 11.0 us)
Async XLA Ops:
  7.2 79.2 %copy-start = (bf16[1024,256]{1,0:T(8,128)(2,1)S(1)}, bf16[1024,256]{1,0:T(8,128)(2,1)}, u32[]{:S(2)}) copy-start(bf16[1024,256]{1,0:T(8,128)(2,1)} %param.18) | copy-start | bytes 1572868
  9.5 3.7 %copy-start.11 = (s32[1,8,1]{1,2,0:T(1,128)S(1)}, s32[1,8,1]{1,2,0:T(1,128)}, u32[]{:S(2)}) copy-start(s32[1,8,1]{1,2,0:T(1,128)} %param.12) | copy-start | bytes 100
  9.5 11.8 %collective-permute-start = (bf16[1,4,8,128]{3,2,1,0:T(8,128)(2,1)S(1)}, bf16[1,4,8,128]{3,2,1,0:T(8,128)(2,1)S(1)}, u32[]{:S(2)}, u32[]{:S(2)}) collective-permute-start(bf16[1,4,8,128]{3,2,1,0:T(8,128)(2,1)S(1)} %bitcast.143), channel_id=1, source_target_pairs={{0,8},{8,16},{16,24},{1,9},{9,17},{17,25},{2,10},{10,18},{18,26},{... | collective-permute-start | bytes 24584 | tf_op jit(solution)/shard_map/ppermute | solution.py:20
  11.9 9.4 %collective-permute-start.1 = (bf16[1,4,8,128]{3,2,1,0:T(8,128)(2,1)S(1)}, bf16[1,4,8,128]{3,2,1,0:T(8,128)(2,1)S(1)}, u32[]{:S(2)}, u32[]{:S(2)}) collective-permute-start(bf16[1,4,8,128]{3,2,1,0:T(8,128)(2,1)S(1)} %bitcast.144), channel_id=1, source_target_pairs={{8,0},{16,8},{24,16},{9,1},{17,9},{25,17},{10,2},{18,10},{26,18},{... | collective-permute-start | bytes 24584 | tf_op jit(solution)/shard_map/ppermute | solution.py:22
  14.4 6.8 %copy-start.10 = (s32[2,8]{1,0:T(2,128)S(1)}, s32[2,8]{1,0:T(2,128)}, u32[]{:S(2)}) copy-start(s32[2,8]{1,0:T(2,128)} %param.11) | copy-start | bytes 196
  14.4 13.3 %all-to-all-start = ((bf16[8,1,8,128]{3,2,1,0:T(8,128)(2,1)}), bf16[8,1,8,128]{3,2,1,0:T(8,128)(2,1)S(1)}, u32[]{:S(2)}, u32[]{:S(2)}) async-start(bf16[8,1,8,128]{3,2,1,0:T(8,128)(2,1)} %bitcast.5), calls=%async_computation | async-start | bytes 32768 | tf_op jit(solution)/shard_map/all_to_all | solution.py:31
  21.1 63.9 %all-gather.2.cloned.1.call-start = ((), (), s32[]{:S(2)}) async-start(), calls=%async_computation.3 | async-start | bytes 1081344 | tf_op jit(solution)/shard_map/all_gather | solution.py:85
  28.3 1.3 copy-start.2
  28.3 1.3 copy-start.3
  28.3 1.3 copy-start.6
  29.6 0.7 copy-start.12
  30.6 0.6 copy-start.7
  86.3 13.2 %copy-start.1 = (bf16[2,8,128,128]{3,2,1,0:T(8,128)(2,1)S(1)}, bf16[2,8,128,128]{3,2,1,0:T(8,128)(2,1)}, u32[]{:S(2)}) copy-start(bf16[2,8,128,128]{3,2,1,0:T(8,128)(2,1)} %param.10) | copy-start | bytes 1572868
  88.0 10.9 %all-to-all-start.1 = ((bf16[8,1,8,128]{3,2,1,0:T(8,128)(2,1)}), bf16[8,1,8,128]{3,2,1,0:T(8,128)(2,1)S(1)}, u32[]{:S(2)}, u32[]{:S(2)}) async-start(bf16[8,1,8,128]{3,2,1,0:T(8,128)(2,1)} %bitcast.21), calls=%async_computation.1 | async-start | bytes 32768 | tf_op jit(solution)/shard_map/all_to_all | solution.py:31
  92.9 3.2 %collective-permute-start.2 = (bf16[1,4,8,128]{3,2,1,0:T(8,128)(2,1)S(1)}, bf16[1,4,8,128]{3,2,1,0:T(8,128)(2,1)S(1)}, u32[]{:S(2)}, u32[]{:S(2)}) collective-permute-start(bf16[1,4,8,128]{3,2,1,0:T(8,128)(2,1)S(1)} %bitcast.147), channel_id=1, source_target_pairs={{0,8},{8,16},{16,24},{1,9},{9,17},{17,25},{2,10},{10,18},{18,26},{... | collective-permute-start | bytes 24584 | tf_op jit(solution)/shard_map/ppermute | solution.py:20
  94.7 3.5 %collective-permute-start.3 = (bf16[1,4,8,128]{3,2,1,0:T(8,128)(2,1)S(1)}, bf16[1,4,8,128]{3,2,1,0:T(8,128)(2,1)S(1)}, u32[]{:S(2)}, u32[]{:S(2)}) collective-permute-start(bf16[1,4,8,128]{3,2,1,0:T(8,128)(2,1)S(1)} %bitcast.148), channel_id=1, source_target_pairs={{8,0},{16,8},{24,16},{9,1},{17,9},{25,17},{10,2},{18,10},{26,18},{... | collective-permute-start | bytes 24584 | tf_op jit(solution)/shard_map/ppermute | solution.py:22
  99.5 0.8 copy-start.5
  100.6 20.0 %copy-start.4 = (bf16[2,8,128]{2,1,0:T(8,128)(2,1)}, bf16[2,8,128]{2,1,0:T(8,128)(2,1)S(1)}, u32[]{:S(2)}) copy-start(bf16[2,8,128]{2,1,0:T(8,128)(2,1)S(1)} %fusion.8) | copy-start | bytes 12292
  102.3 11.1 %collective-permute-start.4 = (bf16[1,4,8,128]{3,2,1,0:T(8,128)(2,1)S(1)}, bf16[1,4,8,128]{3,2,1,0:T(8,128)(2,1)S(1)}, u32[]{:S(2)}, u32[]{:S(2)}) collective-permute-start(bf16[1,4,8,128]{3,2,1,0:T(8,128)(2,1)S(1)} %bitcast.145), channel_id=1, source_target_pairs={{0,8},{8,16},{16,24},{1,9},{9,17},{17,25},{2,10},{10,18},{18,26},{... | collective-permute-start | bytes 24584 | tf_op jit(solution)/shard_map/ppermute | solution.py:20
  105.9 7.4 %collective-permute-start.5 = (bf16[1,4,8,128]{3,2,1,0:T(8,128)(2,1)S(1)}, bf16[1,4,8,128]{3,2,1,0:T(8,128)(2,1)S(1)}, u32[]{:S(2)}, u32[]{:S(2)}) collective-permute-start(bf16[1,4,8,128]{3,2,1,0:T(8,128)(2,1)S(1)} %bitcast.146), channel_id=1, source_target_pairs={{8,0},{16,8},{24,16},{9,1},{17,9},{25,17},{10,2},{18,10},{26,18},{... | collective-permute-start | bytes 24584 | tf_op jit(solution)/shard_map/ppermute | solution.py:22
  107.2 12.6 %all-to-all-start.2 = ((bf16[8,1,8,128]{3,2,1,0:T(8,128)(2,1)}), bf16[8,1,8,128]{3,2,1,0:T(8,128)(2,1)S(1)}, u32[]{:S(2)}, u32[]{:S(2)}) async-start(bf16[8,1,8,128]{3,2,1,0:T(8,128)(2,1)} %bitcast.30), calls=%async_computation.2 | async-start | bytes 32768 | tf_op jit(solution)/shard_map/all_to_all | solution.py:31
  160.2 0.6 copy-start.8
  161.0 0.6 copy-start.9
Sparse Core Ops, SparseCore 0:
  31.3 53.6 all-gather.1
